TPU v7x, 32 devices: a whole 2x2x4 slice. The times are simulated.
32 devices in a mesh: ord: 8 (over z, y), blk: 4 (over x, core).
Axes of the slice: x: 2, y: 2, z: 4, core: 2. Of those that a mesh axis runs over, the one named last changes fastest.
Arguments:
- panel: bfloat16 [2880, 64, 2880], P('ord', 'blk'), as said below
- gauss: bfloat16 [2, 16, 2880, 2880], P(None, None, 'ord', 'blk'), may hold values from -2.3841858e-06 to 2.3841858e-06
- height: float32 [16], replicated, may hold values from 0.25 to 2.5
- order_map: int32 [2880], replicated, may hold values from 0 to 2879, as said below
- cycle_map: int32 [64], P('blk'), may hold values from 360 to 2519, as said below
Outputs:
- field: bfloat16 [5760, 3072], P('ord', 'blk')
Inputs may be any that keep to these rules, and one draw needn't show every extreme that they name: `order_map`: a permutation of 0 to 2879; the 360 slots of each index of ord hold consecutive orders in ascending order. `panel`: entries at degrees below the order of their slot are zero. `cycle_map`: distinct cycle numbers.
All inputs are finite; a program needn't handle non-finite values.
Results may differ from a plain program's by a relative error of at most 0.0068.
Values may be sent and summed in bfloat16 or wider, within the bound.
A program may use at most 256 MiB of HBM per device.

v0:
```python
import math
import jax
import jax.numpy as jnp
from jax import lax
from jax.sharding import PartitionSpec as P

ORDERS = 2880
TILE = 320
NLON = 5760


def cycle_angles(cycle_map):
    theta = math.pi * (cycle_map.astype(jnp.float32) + 0.5) / ORDERS
    return (jnp.cos(theta), jnp.sin(theta))


def legendre_tables(current, before, degree, orders, cosine, sine):
    deg = degree[None, None, :]
    order = orders[:, None, None]
    radial = (deg + 1.0) * current
    polar = (
        -(
            deg * cosine[None, :, None] * current
            - jnp.sqrt(jnp.maximum(deg * deg - order * order, 0.0)) * before
        )
        / sine[None, :, None]
    )
    azimuth = order * current / sine[None, :, None]
    return jnp.stack([radial, polar, azimuth], 2).astype(jnp.bfloat16)


def weighted(coef, degree, height):
    radial = jnp.exp(-(degree[None, :] + 2.0) * height[:, None] / ORDERS)
    return (coef.astype(jnp.float32) * radial[None, :, None, :]).astype(jnp.bfloat16)


def assemble(total, cycles, shells):
    count = total.shape[1]
    parts = total.reshape(2, count, cycles, 3, shells)
    g_part = parts[0]
    h_part = parts[1]
    cosine_part = jnp.concatenate([g_part[:, :, :2], -h_part[:, :, 2:]], 2)
    sine_part = jnp.concatenate([h_part[:, :, :2], g_part[:, :, 2:]], 2)
    return (
        jnp.stack([cosine_part, sine_part])
        .reshape(2, count, cycles * 3 * shells)
        .astype(jnp.bfloat16)
    )


def phase_angles(orders_int, position):
    phase = orders_int[:, None] * position[None, :] % NLON
    angle = phase.astype(jnp.float32) * (2.0 * math.pi / NLON)
    return (jnp.cos(angle), jnp.sin(angle))


def degree_sums(panel_src, edge, coef_src, orders, cosine, sine, height, base, first, last):
    count, cycles, _ = panel_src.shape
    shells = height.shape[0]

    def step(tile, total):
        offset = (tile * TILE - base).astype(jnp.int32)
        current = lax.dynamic_slice_in_dim(panel_src, offset, TILE, 2).astype(jnp.float32)
        earlier = lax.dynamic_slice_in_dim(panel_src, jnp.maximum(offset - 1, 0), TILE, 2).astype(
            jnp.float32
        )
        shifted = jnp.concatenate([edge[:, :, None].astype(jnp.float32), current[:, :, :-1]], 2)
        before = jnp.where(offset > 0, earlier, shifted)
        degree = (tile * TILE + jnp.arange(TILE)).astype(jnp.float32)
        tables = legendre_tables(current, before, degree, orders, cosine, sine).reshape(
            count, cycles * 3, TILE
        )
        weights = weighted(lax.dynamic_slice_in_dim(coef_src, offset, TILE, 3), degree, height)
        return total + jnp.einsum(
            "okl,gsol->goks", tables, weights, preferred_element_type=jnp.float32
        )

    init = jnp.zeros((2, count, cycles * 3, shells), jnp.float32)
    return lax.fori_loop(jnp.asarray(first, jnp.int32), jnp.asarray(last, jnp.int32), step, init)


def body(panel, gauss, height, order_map, cycle_map):
    count, cycles, degrees = panel.shape
    shells = height.shape[0]
    tiles = degrees // TILE
    cosine, sine = cycle_angles(cycle_map)
    coef = lax.all_gather(gauss, "blk", axis=3, tiled=True)
    here = lax.axis_index("ord")
    orders_int = lax.dynamic_slice_in_dim(order_map, here * count, count, 0)
    orders = orders_int.astype(jnp.float32)
    zero_edge = jnp.zeros((count, cycles), jnp.bfloat16)
    total = degree_sums(panel, zero_edge, coef, orders, cosine, sine, height, 0, 0, tiles)
    spectra = assemble(total, cycles, shells)
    spread = lax.all_to_all(spectra, "ord", split_axis=2, concat_axis=1, tiled=True)
    items = spread.shape[2]
    width = NLON // 8
    inner_cos, inner_sin = phase_angles(order_map, jnp.arange(width))
    start_cos, start_sin = phase_angles(order_map, jnp.arange(8) * width)

    def transform(block):
        block_cos = lax.dynamic_slice_in_dim(start_cos, block, 1, 1)
        block_sin = lax.dynamic_slice_in_dim(start_sin, block, 1, 1)
        table_cos = inner_cos * block_cos - inner_sin * block_sin
        table_sin = inner_sin * block_cos + inner_cos * block_sin
        tables = jnp.stack([table_cos, table_sin]).astype(jnp.bfloat16)
        return lax.dot_general(
            tables, spread, (((0, 1), (0, 1)), ((), ())), preferred_element_type=jnp.float32
        )

    field = lax.map(transform, jnp.arange(8)).reshape(NLON, items).astype(jnp.bfloat16)
    return lax.all_to_all(field, "ord", split_axis=0, concat_axis=1, tiled=True)


def solution(mesh):
    return jax.shard_map(
        body,
        mesh=mesh,
        in_specs=(P("ord", "blk", None), P(None, None, "ord", "blk"), P(), P(), P("blk")),
        out_specs=P("ord", "blk"),
        check_vma=False,
    )
```

profile of v0, /device:TPU:0, one launch (start us, length us, event | category | flops | bytes accessed | tf_op | source)
XLA Modules:
  0.0 1558.1 jit_solution(583133086494186010)
XLA Ops:
  6.5 24.1 %copy.29 = bf16[2,16,360,720]{2,1,0,3:T(8,128)(2,1)} copy(bf16[2,16,360,720]{3,2,1,0:T(8,128)(2,1)} %param.10) | data formatting | bytes 33177600 | tf_op args[1]
  31.5 49.6 %copy.31 = bf16[360,16,2880]{0,2,1:T(8,128)(2,1)} copy(bf16[360,16,2880]{2,1,0:T(8,128)(2,1)} %param.9) | data formatting | bytes 66355200
  81.1 367.9 %all-gather.2.cloned.1.call-done = bf16[2,16,360,2880]{2,1,0,3:T(8,128)(2,1)} async-done(((bf16[2,16,360,720]{2,1,0,3:T(8,128)(2,1)}), bf16[2,16,360,2880]{2,1,0,3:T(8,128)(2,1)}) %all-gather.2.cloned.1.call-update) | async-done | bytes 66355216 | tf_op jit(solution)/shard_map/all_gather | solution.py:87
  449.0 670.7 %while.25 = (s32[]{:T(128)}, f32[2,360,48,16]{2,3,0,1:T(8,128)}, bf16[2,16,360,2880]{2,1,0,3:T(8,128)(2,1)}, f32[16]{0:T(128)S(1)}, bf16[360,16,2880]{0,2,1:T(8,...) while((s32[]{:T(128)}, f32[2,360,48,16]{2,3,0,1:T(8,128)}, ...), condition=%wide.region_1.2_spmd.clone, body=%wide.region_0.1_spmd.clone.sunk | while | flops 405015680 | bytes 134444624 | solution.py:79
  471.0 18.0 %copy.44 = bf16[360,48,320,1]{2,1,3,0:T(8,128)(2,1)} copy(bf16[360,48,320,1]{0,2,1,3:T(8,128)(2,1)} %bitcast.76) | data formatting | bytes 22118400 | tf_op jit(solution)/shard_map/while/body/convert_element_type | solution.py:29
  543.1 18.0 %copy.44 = bf16[360,48,320,1]{2,1,3,0:T(8,128)(2,1)} copy(bf16[360,48,320,1]{0,2,1,3:T(8,128)(2,1)} %bitcast.76) | data formatting | bytes 22118400 | tf_op jit(solution)/shard_map/while/body/convert_element_type | solution.py:29
  581.8 14.1 bitcast_add_fusion.2
  617.9 18.0 %copy.44 = bf16[360,48,320,1]{2,1,3,0:T(8,128)(2,1)} copy(bf16[360,48,320,1]{0,2,1,3:T(8,128)(2,1)} %bitcast.76) | data formatting | bytes 22118400 | tf_op jit(solution)/shard_map/while/body/convert_element_type | solution.py:29
  656.6 14.1 bitcast_add_fusion.2
  692.7 18.0 %copy.44 = bf16[360,48,320,1]{2,1,3,0:T(8,128)(2,1)} copy(bf16[360,48,320,1]{0,2,1,3:T(8,128)(2,1)} %bitcast.76) | data formatting | bytes 22118400 | tf_op jit(solution)/shard_map/while/body/convert_element_type | solution.py:29
  731.4 14.1 bitcast_add_fusion.2
  767.5 18.0 %copy.44 = bf16[360,48,320,1]{2,1,3,0:T(8,128)(2,1)} copy(bf16[360,48,320,1]{0,2,1,3:T(8,128)(2,1)} %bitcast.76) | data formatting | bytes 22118400 | tf_op jit(solution)/shard_map/while/body/convert_element_type | solution.py:29
  806.2 14.1 bitcast_add_fusion.2
  842.4 18.0 %copy.44 = bf16[360,48,320,1]{2,1,3,0:T(8,128)(2,1)} copy(bf16[360,48,320,1]{0,2,1,3:T(8,128)(2,1)} %bitcast.76) | data formatting | bytes 22118400 | tf_op jit(solution)/shard_map/while/body/convert_element_type | solution.py:29
  881.1 14.1 bitcast_add_fusion.2
  917.2 18.0 %copy.44 = bf16[360,48,320,1]{2,1,3,0:T(8,128)(2,1)} copy(bf16[360,48,320,1]{0,2,1,3:T(8,128)(2,1)} %bitcast.76) | data formatting | bytes 22118400 | tf_op jit(solution)/shard_map/while/body/convert_element_type | solution.py:29
  955.9 14.1 bitcast_add_fusion.2
  992.1 18.0 %copy.44 = bf16[360,48,320,1]{2,1,3,0:T(8,128)(2,1)} copy(bf16[360,48,320,1]{0,2,1,3:T(8,128)(2,1)} %bitcast.76) | data formatting | bytes 22118400 | tf_op jit(solution)/shard_map/while/body/convert_element_type | solution.py:29
  1030.8 14.1 bitcast_add_fusion.2
  1066.9 18.0 %copy.44 = bf16[360,48,320,1]{2,1,3,0:T(8,128)(2,1)} copy(bf16[360,48,320,1]{0,2,1,3:T(8,128)(2,1)} %bitcast.76) | data formatting | bytes 22118400 | tf_op jit(solution)/shard_map/while/body/convert_element_type | solution.py:29
  1105.6 14.1 bitcast_add_fusion.2
  1135.3 27.8 %all-to-all-done = bf16[2,360,768]{1,0,2:T(2,128)(2,1)S(1)} async-done(((bf16[2,360,768]{1,0,2:T(2,128)(2,1)}), bf16[2,360,768]{1,0,2:T(2,128)(2,1)S(1)}, u32[]{:S(2)}, u32[]{:S(2)}) %all-to-all-start) | async-done | bytes 1105952 | tf_op jit(solution)/shard_map/all_to_all | solution.py:94
  1164.7 352.7 %while.26 = (s32[]{:T(128)}, bf16[8,720,96]{1,2,0:T(8,128)(2,1)S(1)}, s32[8]{0:T(128)S(1)}, f32[2880,8]{0,1:T(8,128)}, f32[2880,8]{0,1:T(8,128)}, /*index=5*/bf1...) while((s32[]{:T(128)}, ...), condition=%wide.region_3.4_spmd.clone.clone, body=%wide.region_2.3_spmd.clone.clone.sunk | while | flops 835660800 | bytes 18279324 | solution.py:110
  1168.2 37.8 %fusion.58 = (bf16[1,2880,720]{1,2,0:T(8,128)(2,1)S(1)}, bf16[1,2880,720]{1,2,0:T(8,128)(2,1)S(1)}) fusion(s32[2880]{0:T(1024)S(1)} %get-tuple-element.493, f32[2880]{0:T(1024)S(1)} %get-tuple-element.418, f32[2880]{0:T(1024)S(1)} %get-tuple-element.419), kind=kLoop, calls=%fused_computation.32.clone.1 | loop fusion | flops 35251200 | bytes 8328960 | tf_op jit(solution)/shard_map/convert
  1212.3 37.8 %fusion.58 = (bf16[1,2880,720]{1,2,0:T(8,128)(2,1)S(1)}, bf16[1,2880,720]{1,2,0:T(8,128)(2,1)S(1)}) fusion(s32[2880]{0:T(1024)S(1)} %get-tuple-element.493, f32[2880]{0:T(1024)S(1)} %get-tuple-element.418, f32[2880]{0:T(1024)S(1)} %get-tuple-element.419), kind=kLoop, calls=%fused_computation.32.clone.1 | loop fusion | flops 35251200 | bytes 8328960 | tf_op jit(solution)/shard_map/convert
  1256.4 37.8 %fusion.58 = (bf16[1,2880,720]{1,2,0:T(8,128)(2,1)S(1)}, bf16[1,2880,720]{1,2,0:T(8,128)(2,1)S(1)}) fusion(s32[2880]{0:T(1024)S(1)} %get-tuple-element.493, f32[2880]{0:T(1024)S(1)} %get-tuple-element.418, f32[2880]{0:T(1024)S(1)} %get-tuple-element.419), kind=kLoop, calls=%fused_computation.32.clone.1 | loop fusion | flops 35251200 | bytes 8328960 | tf_op jit(solution)/shard_map/convert
  1300.5 37.8 %fusion.58 = (bf16[1,2880,720]{1,2,0:T(8,128)(2,1)S(1)}, bf16[1,2880,720]{1,2,0:T(8,128)(2,1)S(1)}) fusion(s32[2880]{0:T(1024)S(1)} %get-tuple-element.493, f32[2880]{0:T(1024)S(1)} %get-tuple-element.418, f32[2880]{0:T(1024)S(1)} %get-tuple-element.419), kind=kLoop, calls=%fused_computation.32.clone.1 | loop fusion | flops 35251200 | bytes 8328960 | tf_op jit(solution)/shard_map/convert
  1344.6 37.8 %fusion.58 = (bf16[1,2880,720]{1,2,0:T(8,128)(2,1)S(1)}, bf16[1,2880,720]{1,2,0:T(8,128)(2,1)S(1)}) fusion(s32[2880]{0:T(1024)S(1)} %get-tuple-element.493, f32[2880]{0:T(1024)S(1)} %get-tuple-element.418, f32[2880]{0:T(1024)S(1)} %get-tuple-element.419), kind=kLoop, calls=%fused_computation.32.clone.1 | loop fusion | flops 35251200 | bytes 8328960 | tf_op jit(solution)/shard_map/convert
  1388.7 37.8 %fusion.58 = (bf16[1,2880,720]{1,2,0:T(8,128)(2,1)S(1)}, bf16[1,2880,720]{1,2,0:T(8,128)(2,1)S(1)}) fusion(s32[2880]{0:T(1024)S(1)} %get-tuple-element.493, f32[2880]{0:T(1024)S(1)} %get-tuple-element.418, f32[2880]{0:T(1024)S(1)} %get-tuple-element.419), kind=kLoop, calls=%fused_computation.32.clone.1 | loop fusion | flops 35251200 | bytes 8328960 | tf_op jit(solution)/shard_map/convert
  1432.8 37.8 %fusion.58 = (bf16[1,2880,720]{1,2,0:T(8,128)(2,1)S(1)}, bf16[1,2880,720]{1,2,0:T(8,128)(2,1)S(1)}) fusion(s32[2880]{0:T(1024)S(1)} %get-tuple-element.493, f32[2880]{0:T(1024)S(1)} %get-tuple-element.418, f32[2880]{0:T(1024)S(1)} %get-tuple-element.419), kind=kLoop, calls=%fused_computation.32.clone.1 | loop fusion | flops 35251200 | bytes 8328960 | tf_op jit(solution)/shard_map/convert
  1476.9 37.8 %fusion.58 = (bf16[1,2880,720]{1,2,0:T(8,128)(2,1)S(1)}, bf16[1,2880,720]{1,2,0:T(8,128)(2,1)S(1)}) fusion(s32[2880]{0:T(1024)S(1)} %get-tuple-element.493, f32[2880]{0:T(1024)S(1)} %get-tuple-element.418, f32[2880]{0:T(1024)S(1)} %get-tuple-element.419), kind=kLoop, calls=%fused_computation.32.clone.1 | loop fusion | flops 35251200 | bytes 8328960 | tf_op jit(solution)/shard_map/convert
  1517.4 32.5 %all_to_all.34 = bf16[8,720,96]{1,2,0:T(8,128)(2,1)S(1)} all-to-all(bf16[8,720,96]{1,2,0:T(8,128)(2,1)S(1)} %get-tuple-element.155), channel_id=1, replica_groups=mesh['ord'=8,'blk'=4] {'ord'}, dimensions={0} | all-to-all | bytes 2211840 | tf_op jit(solution)/shard_map/all_to_all | solution.py:111
  (156 shorter events, 449.4 us)
Async XLA Ops:
  6.5 442.5 %all-gather.2.cloned.1.call-start = ((), (), s32[]{:S(2)}) async-start(), calls=%async_computation.2 | async-start | bytes 88473600 | tf_op jit(solution)/shard_map/all_gather | solution.py:87
  31.4 49.6 %copy-start.2 = (s32[16]{0:T(128)S(1)}, s32[16]{0:T(128)}, u32[]{:S(2)}) copy-start(s32[16]{0:T(128)} %param.13) | copy-start | bytes 196
  31.5 417.6 %copy-start.1 = (f32[16]{0:T(128)S(1)}, f32[16]{0:T(128)}, u32[]{:S(2)}) copy-start(f32[16]{0:T(128)} %param.11) | copy-start | bytes 196
  1125.6 8.6 copy-start
  1128.6 34.5 %all-to-all-start = ((bf16[2,360,768]{1,0,2:T(2,128)(2,1)}), bf16[2,360,768]{1,0,2:T(2,128)(2,1)S(1)}, u32[]{:S(2)}, u32[]{:S(2)}) async-start(bf16[2,360,768]{1,0,2:T(2,128)(2,1)} %copy.34), calls=%async_computation | async-start | bytes 2359296 | tf_op jit(solution)/shard_map/all_to_all | solution.py:94
Sparse Core Ops, SparseCore 0:
  30.8 418.2 all-gather.1
where the time goes:
time: 1570 us; the launch traced here: 1560 us
  other arithmetic  503 us (32%)
  local copies, waits for them, and re-layouts  446 us (28%)
  waiting for transfers between devices  396 us (25%)
  matrix products  146 us (9%)
  blocking collectives  32.5 us (2%)
    all_gather x1, waiting for transfers between devices, body(): coef = lax.all_gather(gauss, 'blk', axis=3, tiled=True)  368 us
    another operation x9, other arithmetic  303 us
    dynamic_slice x18, local copies, waits for them, and re-layouts, step(): lax.dynamic_slice_in_dim(coef_src, offset, TILE, 3)  186 us
    convert_element_type x9, local copies, waits for them, and re-layouts, legendre_tables(): return jnp.stack([radial, polar, azimuth], 2).astype(jnp.bfloat16)  162 us
    another operation x18, other arithmetic, legendre_tables(): return jnp.stack([radial, polar, azimuth], 2).astype(jnp.bfloat16)  141 us
    dot_general x9, matrix products, step(): jnp.einsum('okl,gsol->goks', tables, weights, preferred_element_type=jnp....  124 us
    unnamed x8, local copies, waits for them, and re-layouts  73.7 us
    convert_element_type x9, other arithmetic, step(): lax.dynamic_slice_in_dim(panel_src, offset, TILE, 2).astype(jnp.float32)  54.1 us
  transfers between devices with their start and end apart: 2, of which 2 were waited for; matrix products, arithmetic and copies ran while one was open for 3% of the time, Pallas kernels for 0%

commit v1 on v0

--- a/solution.py
+++ b/solution.py
@@ -84,7 +84,8 @@
     shells = height.shape[0]
     tiles = degrees // TILE
     cosine, sine = cycle_angles(cycle_map)
-    coef = lax.all_gather(gauss, "blk", axis=3, tiled=True)
+    shards = lax.all_gather(gauss, "blk")
+    coef = jnp.concatenate(shards, axis=3)
     here = lax.axis_index("ord")
     orders_int = lax.dynamic_slice_in_dim(order_map, here * count, count, 0)
     orders = orders_int.astype(jnp.float32)

time: 1570 us -> 1540 us (0.981)
  other arithmetic: 503 us -> 457 us
    reshape x0 -> x2, local copies, waits for them, and re-layouts: none -> 215 us  [body(): coef = jnp.concatenate(shards, axis=3)]
    dynamic_slice x18 -> x0, local copies, waits for them, and re-layouts: 186 us -> none  [step(): lax.dynamic_slice_in_dim(coef_src, offset, TILE, 3)]
    convert_element_type x9, other arithmetic: 54.1 us -> 26.4 us  [step(): lax.dynamic_slice_in_dim(panel_src, offset, TILE, 2).astype(jnp.float32)]
    unnamed x8 -> x7, local copies, waits for them, and re-layouts: 73.7 us -> 49.9 us
    another operation x18, other arithmetic: 141 us -> 122 us  [legendre_tables(): return jnp.stack([radial, polar, azimuth], 2).astype(jnp.bfloat16)]
where the time goes in v1:
time: 1540 us; the launch traced here: 1530 us
  other arithmetic  457 us (30%)
  local copies, waits for them, and re-layouts  450 us (29%)
  waiting for transfers between devices  398 us (26%)
  matrix products  154 us (10%)
  blocking collectives  32.5 us (2%)
  loops' own time  15.7 us (1%)
    all_gather x1, waiting for transfers between devices, body(): shards = lax.all_gather(gauss, 'blk')  369 us
    another operation x9, other arithmetic  303 us
    reshape x2, local copies, waits for them, and re-layouts, body(): coef = jnp.concatenate(shards, axis=3)  215 us
    convert_element_type x9, local copies, waits for them, and re-layouts, legendre_tables(): return jnp.stack([radial, polar, azimuth], 2).astype(jnp.bfloat16)  161 us
    dot_general x9, matrix products, step(): jnp.einsum('okl,gsol->goks', tables, weights, preferred_element_type=jnp....  132 us
    another operation x18, other arithmetic, legendre_tables(): return jnp.stack([radial, polar, azimuth], 2).astype(jnp.bfloat16)  122 us
    unnamed x7, local copies, waits for them, and re-layouts  49.9 us
    all_to_all x1, blocking collectives, body(): return lax.all_to_all(field, 'ord', split_axis=0, concat_axis=1, tiled=True)  32.5 us
  transfers between devices with their start and end apart: 2, of which 2 were waited for; matrix products, arithmetic and copies ran while one was open for 3% of the time, Pallas kernels for 0%

profile of v1, /device:TPU:0, one launch (start us, length us, event | category | flops | bytes accessed | tf_op | source)
XLA Modules:
  0.0 1525.9 jit_solution(3254513842809596323)
XLA Ops:
  8.1 49.9 %copy.30 = bf16[360,16,2880]{0,2,1:T(8,128)(2,1)} copy(bf16[360,16,2880]{2,1,0:T(8,128)(2,1)} %param.9) | data formatting | bytes 66355200
  58.0 369.2 %all-gather.3.cloned.1.call-done = bf16[8,16,360,720]{3,2,1,0:T(8,128)(2,1)} async-done(((bf16[2,16,360,720]{3,2,1,0:T(8,128)(2,1)}), bf16[8,16,360,720]{3,2,1,0:T(8,128)(2,1)}) %all-gather.3.cloned.1.call-update) | async-done | bytes 66355216 | tf_op jit(solution)/shard_map/all_gather | solution.py:87
  427.2 88.9 %copy.29 = bf16[2,16,360,4,720]{4,3,1,0,2:T(4,128)(2,1)} copy(bf16[2,16,360,4,720]{4,2,1,0,3:T(8,128)(2,1)} %bitcast.1) | data formatting | bytes 132710400 | tf_op jit(solution)/shard_map/reshape | solution.py:88
  516.0 125.7 %reshape.313 = bf16[2,16,360,2880]{3,1,0,2:T(8,128)(2,1)} reshape(bf16[2,16,360,4,720]{4,3,1,0,2:T(4,128)(2,1)} %copy.29) | data formatting | bytes 132710400 | tf_op jit(solution)/shard_map/reshape | solution.py:88
  641.7 445.8 %while.25 = (s32[]{:T(128)}, f32[2,360,48,16]{2,3,0,1:T(8,128)}, bf16[2,16,360,2880]{3,1,0,2:T(8,128)(2,1)}, f32[16]{0:T(128)S(1)}, bf16[360,16,2880]{0,2,1:T(8,...) while((s32[]{:T(128)}, f32[2,360,48,16]{2,3,0,1:T(8,128)}, ...), condition=%wide.region_1.2_spmd.clone, body=%wide.region_0.1_spmd.clone.sunk | while | flops 405015680 | bytes 112326224 | solution.py:79
  658.8 17.9 %copy.41 = bf16[360,48,320,1]{2,1,3,0:T(8,128)(2,1)} copy(bf16[360,48,320,1]{0,2,1,3:T(8,128)(2,1)} %bitcast.81) | data formatting | bytes 22118400 | tf_op jit(solution)/shard_map/while/body/convert_element_type | solution.py:29
  706.0 17.9 %copy.41 = bf16[360,48,320,1]{2,1,3,0:T(8,128)(2,1)} copy(bf16[360,48,320,1]{0,2,1,3:T(8,128)(2,1)} %bitcast.81) | data formatting | bytes 22118400 | tf_op jit(solution)/shard_map/while/body/convert_element_type | solution.py:29
  723.9 15.1 bitcast_add_fusion.2
  755.9 17.9 %copy.41 = bf16[360,48,320,1]{2,1,3,0:T(8,128)(2,1)} copy(bf16[360,48,320,1]{0,2,1,3:T(8,128)(2,1)} %bitcast.81) | data formatting | bytes 22118400 | tf_op jit(solution)/shard_map/while/body/convert_element_type | solution.py:29
  773.8 15.1 bitcast_add_fusion.2
  805.7 17.9 %copy.41 = bf16[360,48,320,1]{2,1,3,0:T(8,128)(2,1)} copy(bf16[360,48,320,1]{0,2,1,3:T(8,128)(2,1)} %bitcast.81) | data formatting | bytes 22118400 | tf_op jit(solution)/shard_map/while/body/convert_element_type | solution.py:29
  823.7 15.1 bitcast_add_fusion.2
  855.7 17.9 %copy.41 = bf16[360,48,320,1]{2,1,3,0:T(8,128)(2,1)} copy(bf16[360,48,320,1]{0,2,1,3:T(8,128)(2,1)} %bitcast.81) | data formatting | bytes 22118400 | tf_op jit(solution)/shard_map/while/body/convert_element_type | solution.py:29
  873.6 15.1 bitcast_add_fusion.2
  905.6 17.9 %copy.41 = bf16[360,48,320,1]{2,1,3,0:T(8,128)(2,1)} copy(bf16[360,48,320,1]{0,2,1,3:T(8,128)(2,1)} %bitcast.81) | data formatting | bytes 22118400 | tf_op jit(solution)/shard_map/while/body/convert_element_type | solution.py:29
  923.6 15.1 bitcast_add_fusion.2
  955.5 17.9 %copy.41 = bf16[360,48,320,1]{2,1,3,0:T(8,128)(2,1)} copy(bf16[360,48,320,1]{0,2,1,3:T(8,128)(2,1)} %bitcast.81) | data formatting | bytes 22118400 | tf_op jit(solution)/shard_map/while/body/convert_element_type | solution.py:29
  973.4 15.1 bitcast_add_fusion.2
  1005.4 17.9 %copy.41 = bf16[360,48,320,1]{2,1,3,0:T(8,128)(2,1)} copy(bf16[360,48,320,1]{0,2,1,3:T(8,128)(2,1)} %bitcast.81) | data formatting | bytes 22118400 | tf_op jit(solution)/shard_map/while/body/convert_element_type | solution.py:29
  1023.3 15.1 bitcast_add_fusion.2
  1055.3 17.9 %copy.41 = bf16[360,48,320,1]{2,1,3,0:T(8,128)(2,1)} copy(bf16[360,48,320,1]{0,2,1,3:T(8,128)(2,1)} %bitcast.81) | data formatting | bytes 22118400 | tf_op jit(solution)/shard_map/while/body/convert_element_type | solution.py:29
  1103.0 27.8 %all-to-all-done = bf16[2,360,768]{1,0,2:T(2,128)(2,1)S(1)} async-done(((bf16[2,360,768]{1,0,2:T(2,128)(2,1)}), bf16[2,360,768]{1,0,2:T(2,128)(2,1)S(1)}, u32[]{:S(2)}, u32[]{:S(2)}) %all-to-all-start) | async-done | bytes 1105952 | tf_op jit(solution)/shard_map/all_to_all | solution.py:95
  1132.4 352.7 %while.26 = (s32[]{:T(128)}, bf16[8,720,96]{1,2,0:T(8,128)(2,1)S(1)}, s32[8]{0:T(128)S(1)}, f32[2880,8]{0,1:T(8,128)}, f32[2880,8]{0,1:T(8,128)}, /*index=5*/bf1...) while((s32[]{:T(128)}, ...), condition=%wide.region_3.4_spmd.clone.clone, body=%wide.region_2.3_spmd.clone.clone.sunk | while | flops 835660800 | bytes 18279332 | solution.py:111
  1135.9 37.8 %fusion.60 = (bf16[1,2880,720]{1,2,0:T(8,128)(2,1)S(1)}, bf16[1,2880,720]{1,2,0:T(8,128)(2,1)S(1)}) fusion(s32[2880]{0:T(1024)S(1)} %get-tuple-element.493, f32[2880]{0:T(1024)S(1)} %get-tuple-element.418, f32[2880]{0:T(1024)S(1)} %get-tuple-element.419), kind=kLoop, calls=%fused_computation.33.clone.1 | loop fusion | flops 35251200 | bytes 8328960 | tf_op jit(solution)/shard_map/convert
  1180.0 37.8 %fusion.60 = (bf16[1,2880,720]{1,2,0:T(8,128)(2,1)S(1)}, bf16[1,2880,720]{1,2,0:T(8,128)(2,1)S(1)}) fusion(s32[2880]{0:T(1024)S(1)} %get-tuple-element.493, f32[2880]{0:T(1024)S(1)} %get-tuple-element.418, f32[2880]{0:T(1024)S(1)} %get-tuple-element.419), kind=kLoop, calls=%fused_computation.33.clone.1 | loop fusion | flops 35251200 | bytes 8328960 | tf_op jit(solution)/shard_map/convert
  1224.1 37.8 %fusion.60 = (bf16[1,2880,720]{1,2,0:T(8,128)(2,1)S(1)}, bf16[1,2880,720]{1,2,0:T(8,128)(2,1)S(1)}) fusion(s32[2880]{0:T(1024)S(1)} %get-tuple-element.493, f32[2880]{0:T(1024)S(1)} %get-tuple-element.418, f32[2880]{0:T(1024)S(1)} %get-tuple-element.419), kind=kLoop, calls=%fused_computation.33.clone.1 | loop fusion | flops 35251200 | bytes 8328960 | tf_op jit(solution)/shard_map/convert
  1268.2 37.8 %fusion.60 = (bf16[1,2880,720]{1,2,0:T(8,128)(2,1)S(1)}, bf16[1,2880,720]{1,2,0:T(8,128)(2,1)S(1)}) fusion(s32[2880]{0:T(1024)S(1)} %get-tuple-element.493, f32[2880]{0:T(1024)S(1)} %get-tuple-element.418, f32[2880]{0:T(1024)S(1)} %get-tuple-element.419), kind=kLoop, calls=%fused_computation.33.clone.1 | loop fusion | flops 35251200 | bytes 8328960 | tf_op jit(solution)/shard_map/convert
  1312.3 37.8 %fusion.60 = (bf16[1,2880,720]{1,2,0:T(8,128)(2,1)S(1)}, bf16[1,2880,720]{1,2,0:T(8,128)(2,1)S(1)}) fusion(s32[2880]{0:T(1024)S(1)} %get-tuple-element.493, f32[2880]{0:T(1024)S(1)} %get-tuple-element.418, f32[2880]{0:T(1024)S(1)} %get-tuple-element.419), kind=kLoop, calls=%fused_computation.33.clone.1 | loop fusion | flops 35251200 | bytes 8328960 | tf_op jit(solution)/shard_map/convert
  1356.4 37.8 %fusion.60 = (bf16[1,2880,720]{1,2,0:T(8,128)(2,1)S(1)}, bf16[1,2880,720]{1,2,0:T(8,128)(2,1)S(1)}) fusion(s32[2880]{0:T(1024)S(1)} %get-tuple-element.493, f32[2880]{0:T(1024)S(1)} %get-tuple-element.418, f32[2880]{0:T(1024)S(1)} %get-tuple-element.419), kind=kLoop, calls=%fused_computation.33.clone.1 | loop fusion | flops 35251200 | bytes 8328960 | tf_op jit(solution)/shard_map/convert
  1400.5 37.8 %fusion.60 = (bf16[1,2880,720]{1,2,0:T(8,128)(2,1)S(1)}, bf16[1,2880,720]{1,2,0:T(8,128)(2,1)S(1)}) fusion(s32[2880]{0:T(1024)S(1)} %get-tuple-element.493, f32[2880]{0:T(1024)S(1)} %get-tuple-element.418, f32[2880]{0:T(1024)S(1)} %get-tuple-element.419), kind=kLoop, calls=%fused_computation.33.clone.1 | loop fusion | flops 35251200 | bytes 8328960 | tf_op jit(solution)/shard_map/convert
  1444.6 37.8 %fusion.60 = (bf16[1,2880,720]{1,2,0:T(8,128)(2,1)S(1)}, bf16[1,2880,720]{1,2,0:T(8,128)(2,1)S(1)}) fusion(s32[2880]{0:T(1024)S(1)} %get-tuple-element.493, f32[2880]{0:T(1024)S(1)} %get-tuple-element.418, f32[2880]{0:T(1024)S(1)} %get-tuple-element.419), kind=kLoop, calls=%fused_computation.33.clone.1 | loop fusion | flops 35251200 | bytes 8328960 | tf_op jit(solution)/shard_map/convert
  1485.1 32.5 %all_to_all.34 = bf16[8,720,96]{1,2,0:T(8,128)(2,1)S(1)} all-to-all(bf16[8,720,96]{1,2,0:T(8,128)(2,1)S(1)} %get-tuple-element.155), channel_id=1, replica_groups=mesh['ord'=8,'blk'=4] {'ord'}, dimensions={0} | all-to-all | bytes 2211840 | tf_op jit(solution)/shard_map/all_to_all | solution.py:112
  (139 shorter events, 233.2 us)
Async XLA Ops:
  6.5 420.6 %all-gather.3.cloned.1.call-start = ((), (), s32[]{:S(2)}) async-start(), calls=%async_computation.2 | async-start | bytes 88473600 | tf_op jit(solution)/shard_map/all_gather | solution.py:87
  8.1 49.9 %copy-start.2 = (s32[16]{0:T(128)S(1)}, s32[16]{0:T(128)}, u32[]{:S(2)}) copy-start(s32[16]{0:T(128)} %param.13) | copy-start | bytes 196
  516.0 125.7 %copy-start.1 = (f32[16]{0:T(128)S(1)}, f32[16]{0:T(128)}, u32[]{:S(2)}) copy-start(f32[16]{0:T(128)} %param.11) | copy-start | bytes 196
  1093.3 8.6 copy-start
  1096.3 34.5 %all-to-all-start = ((bf16[2,360,768]{1,0,2:T(2,128)(2,1)}), bf16[2,360,768]{1,0,2:T(2,128)(2,1)S(1)}, u32[]{:S(2)}, u32[]{:S(2)}) async-start(bf16[2,360,768]{1,0,2:T(2,128)(2,1)} %copy.33), calls=%async_computation | async-start | bytes 2359296 | tf_op jit(solution)/shard_map/all_to_all | solution.py:95
Sparse Core Ops, SparseCore 0:
  8.9 418.1 all-gather.2
